TPU v7x, 32 devices: a whole 2x2x4 slice. The times are simulated.
32 devices in a mesh: dp: 4 (over y, core), tensor: 2 (over x), pipe: 4 (over z).
Axes of the slice: x: 2, y: 2, z: 4, core: 2. Of those that a mesh axis runs over, the one named last changes fastest.
Arguments:
- grad_parts: float32 [4, 4, 2, 64, 8192], P('dp', 'pipe', 'tensor'), may hold values from -24 to 24
- drop_flags: int32 [4, 4, 2, 64], P('dp', 'pipe', 'tensor'), may hold values from 0 to 1, as said below
- owner_order: int32 [4], replicated, may hold values from 0 to 3, each once
- step_count: int32 [], replicated, may hold values from 1 to 11
- master: float32 [4, 2, 64, 8192], P('pipe', 'tensor', None, 'dp'), may hold values from -6 to 6
- moment_m: float32 [4, 2, 64, 8192], P('pipe', 'tensor', None, 'dp'), may hold values from -0.15625 to 0.15625
- moment_v: float32 [4, 2, 64, 8192], P('pipe', 'tensor', None, 'dp'), may hold values from 0.0001 to 0.001
Outputs:
- new_master: float32 [4, 2, 64, 8192], P('pipe', 'tensor', None, 'dp')
- new_m: float32 [4, 2, 64, 8192], P('pipe', 'tensor', None, 'dp')
- new_v: float32 [4, 2, 64, 8192], P('pipe', 'tensor', None, 'dp')
- direction: float32 [4, 2, 64, 8192], P('pipe', 'tensor', None, 'dp')
- dropped_total: int32 [], replicated
Inputs may be any that keep to these rules, and one draw needn't show every extreme that they name: `drop_flags`: A row may be flagged by every replica.
All inputs are finite; a program needn't handle non-finite values.
Results may differ from a plain program's by a relative error of at most 0.0003.
Values sent between devices are 32-bit elements; how exact they have to be, the bound alone decides.
A program may use at most 64 MiB of HBM per device.

v0:
```python
import jax
import jax.numpy as jnp
from jax import lax
from jax.sharding import PartitionSpec as P


def body(grad_parts, drop_flags, owner_order, step_count, master, moment_m, moment_v):
    replicas = lax.axis_size("dp")
    flags = drop_flags[0, 0, 0]
    kept = (1 - flags).astype(jnp.float32)
    local_grad = grad_parts[0, 0, 0]
    rows_here = local_grad.shape[0]
    width = local_grad.shape[1]
    block_cols = width // replicas
    term = local_grad * kept[:, None]
    blocks = jnp.take(term.reshape(rows_here, replicas, block_cols), owner_order, axis=1)
    received = lax.all_to_all(blocks, "dp", split_axis=1, concat_axis=1, tiled=True)
    summed = jnp.sum(received, axis=1)
    count = lax.psum(kept, "dp")
    grad = summed / jnp.maximum(count, 1.0)[:, None]
    square_sum, dropped = lax.psum(
        (jnp.sum(grad * grad), jnp.sum(flags).astype(jnp.float32)), ("dp", "tensor", "pipe")
    )
    entries = rows_here * width * lax.axis_size("tensor") * lax.axis_size("pipe")
    rms = jnp.sqrt(square_sum / entries)
    clip = jnp.minimum(1.0, 0.05 / (rms + 1e-06))
    scaled = clip * grad
    old_m = moment_m[0, 0]
    old_v = moment_v[0, 0]
    weights = master[0, 0]
    new_m = 0.9 * old_m + 0.1 * scaled
    new_v = 0.999 * old_v + 0.001 * scaled * scaled
    steps = step_count.astype(jnp.float32)
    m_hat = new_m / (1.0 - jnp.power(0.9, steps))
    v_hat = new_v / (1.0 - jnp.power(0.999, steps))
    direction = m_hat / (jnp.sqrt(v_hat) + 1e-08) + 0.1 * weights
    new_master = weights - 0.001 * direction
    return (
        new_master[None, None],
        new_m[None, None],
        new_v[None, None],
        direction[None, None],
        dropped.astype(jnp.int32),
    )


def solution(mesh):
    return jax.shard_map(
        body,
        mesh=mesh,
        in_specs=(
            P("dp", "pipe", "tensor", None, None),
            P("dp", "pipe", "tensor", None),
            P(),
            P(),
            P("pipe", "tensor", None, "dp"),
            P("pipe", "tensor", None, "dp"),
            P("pipe", "tensor", None, "dp"),
        ),
        out_specs=(
            P("pipe", "tensor", None, "dp"),
            P("pipe", "tensor", None, "dp"),
            P("pipe", "tensor", None, "dp"),
            P("pipe", "tensor", None, "dp"),
            P(),
        ),
        check_vma=False,
    )
```

profile of v0, /device:TPU:0, one launch (start us, length us, event | category | flops | bytes accessed | tf_op | source)
XLA Modules:
  0.0 91.8 jit_solution(3209272403787313384)
XLA Ops:
  0.6 0.7 compare_select_fusion
  1.3 0.7 compare_and_fusion
  2.0 1.3 %fusion.3 = (s32[]{:T(128)}, f32[64]{0:T(128)S(1)}) fusion(s32[1,1,1,64]{3,2,1,0:T(1,128)} %param.8), kind=kLoop, calls=%fused_computation.16 | loop fusion | flops 191 | bytes 516 | tf_op jit(solution)/shard_map/reduce_sum | solution.py:22
  3.2 2.7 %squeeze.2 = f32[64,4,2048]{2,1,0:T(4,128)S(1)} reshape(f32[1,1,1,64,8192]{4,3,2,1,0:T(8,128)} %param.7) | data formatting | bytes 4194304 | tf_op jit(solution)/shard_map/squeeze | solution.py:11
  5.9 2.6 %copy_multiply_fusion = f32[64,4,2048]{2,0,1:T(8,128)} fusion(f32[64,4,2048]{2,1,0:T(4,128)S(1)} %squeeze.2, f32[64]{0:T(128)S(1)} %get-tuple-element.12), kind=kLoop, calls=%fused_computation.1 | loop fusion | flops 524288 | bytes 4194560 | tf_op jit(solution)/shard_map/mul | solution.py:15
  8.5 2.3 %gather_fusion = f32[4,64,2048]{2,1,0:T(8,128)S(1)} fusion(f32[64,4,2048]{2,0,1:T(8,128)} %copy_multiply_fusion, s32[1024]{0:T(1024)S(1)} %pad_clamp_fusion), kind=kCustom, calls=%fused_computation | custom fusion | bytes 4194320 | tf_op jit(solution)/shard_map/jit(_take)/gather | solution.py:16
  10.8 1.6 %select_bitcast_fusion = f32[64,4,2048]{2,0,1:T(8,128)} fusion(f32[4,64,2048]{2,1,0:T(8,128)S(1)} %gather_fusion, pred[4]{0:T(512)(128)(4,1)S(1)} %compare_and_fusion), kind=kLoop, calls=%fused_computation.2 | loop fusion | flops 524288 | bytes 4194308 | tf_op jit(solution)/shard_map/jit(_take)/select_n | solution.py:16
  12.4 4.3 %all-to-all-start = ((f32[64,4,2048]{2,0,1:T(8,128)}), f32[64,4,2048]{2,0,1:T(8,128)S(1)}, u32[]{:S(2)}, u32[]{:S(2)}) async-start(f32[64,4,2048]{2,0,1:T(8,128)} %select_bitcast_fusion), calls=%async_computation | async-start | bytes 4194304 | tf_op jit(solution)/shard_map/all_to_all | solution.py:17
  16.7 0.0 copy-start
  18.1 25.7 %psum.21 = f32[64]{0:T(128)S(1)} all-reduce(f32[64]{0:T(128)S(1)} %get-tuple-element.12), channel_id=1, replica_groups=mesh['dp'=4,'tensor'=2,'pipe'=4] {'dp'}, use_global_device_ids=true, to_apply=%region_1.2 | all-reduce | flops 64 | bytes 512 | tf_op jit(solution)/shard_map/psum | solution.py:19
  43.8 0.0 all-to-all-done
  43.8 0.2 reduce_sum.29
  44.0 0.8 multiply_reduce_fusion
  44.8 41.6 %all-reduce = (f32[]{:T(128)}, f32[]{:T(128)}) all-reduce(f32[]{:T(128)} %multiply_reduce_fusion, f32[]{:T(128)S(6)} %convert_element_type.22), channel_id=1, replica_groups=mesh['dp'=4,'tensor'=2,'pipe'=4] {'dp','tensor','pipe'}, use_global_device_ids=true, to_apply=%region_3.4 | all-reduce | flops 2 | bytes 16 | tf_op jit(solution)/shard_map/psum | solution.py:21
  87.8 0.0 copy-done
  87.8 2.9 %multiply_subtract_fusion = (f32[1,1,64,2048]{3,2,1,0:T(8,128)}, f32[1,1,64,2048]{3,2,1,0:T(8,128)}, f32[1,1,64,2048]{3,2,1,0:T(8,128)}, f32[1,1,64,2048]{3,2,1,0:T(8,128)}) fusion(f32[1,1,64,2048]{3,2,1,0:T(8,128)S(1)} %copy-done, f32[]{:T(128)S(6)} %sub.24, f32[]{:T(128)S(6)} %sub.23, f32[64]{0:T(128)S(1)} %broadcast_maximum_fusion, ...), kind=kLoop, calls=%fused_computation.7 | loop fusion | flops 2228224 | bytes 4194572 | tf_op jit(solution)/shard_map/sub | solution.py:37
  (2 shorter events, 0.0 us)
Async XLA Ops:
  12.4 31.4 %all-to-all-start = ((f32[64,4,2048]{2,0,1:T(8,128)}), f32[64,4,2048]{2,0,1:T(8,128)S(1)}, u32[]{:S(2)}, u32[]{:S(2)}) async-start(f32[64,4,2048]{2,0,1:T(8,128)} %select_bitcast_fusion), calls=%async_computation | async-start | bytes 4194304 | tf_op jit(solution)/shard_map/all_to_all | solution.py:17
  16.7 71.1 %copy-start = (f32[1,1,64,2048]{3,2,1,0:T(8,128)S(1)}, f32[1,1,64,2048]{3,2,1,0:T(8,128)}, u32[]{:S(2)}) copy-start(f32[1,1,64,2048]{3,2,1,0:T(8,128)} %param.11) | copy-start | bytes 1572868
where the time goes:
time: 92.3 us; the launch traced here: 91.8 us
  blocking collectives  67.3 us (73%)
  other arithmetic  10.7 us (12%)
  local copies, waits for them, and re-layouts  4.94 us (5%)
  between operations  4.63 us (5%)
  starting transfers between devices  4.26 us (5%)
    psum x1, blocking collectives, body(): lax.psum((jnp.sum(grad * grad), jnp.sum(flags).astype(jnp.float32)), ('dp...  41.6 us
    psum x1, blocking collectives, body(): count = lax.psum(kept, 'dp')  25.7 us
    all_to_all x1, starting transfers between devices, body(): lax.all_to_all(blocks, 'dp', split_axis=1, concat_axis=1, tiled=True)  4.26 us
    sub x1, other arithmetic, body(): new_master = weights - 0.001 * direction  2.86 us
    squeeze x1, local copies, waits for them, and re-layouts, body(): local_grad = grad_parts[0, 0, 0]  2.67 us
    mul x1, other arithmetic, body(): term = local_grad * kept[:, None]  2.57 us
    select_n x2, other arithmetic, body(): jnp.take(term.reshape(rows_here, replicas, block_cols), owner_order, axis=1)  2.3 us
    gather x1, local copies, waits for them, and re-layouts, body(): jnp.take(term.reshape(rows_here, replicas, block_cols), owner_order, axis=1)  2.27 us
  transfers between devices with their start and end apart: 1, of which 0 were waited for; matrix products, arithmetic and copies ran while one was open for 0% of the time, Pallas kernels for 0%

commit v1 on v0

v1 whole, which is shorter than its diff:
```python
import functools
import itertools
import jax
import jax.numpy as jnp
from jax import lax
from jax.experimental import pallas as pl
from jax.experimental.pallas import tpu as pltpu
from jax.sharding import PartitionSpec as P

AXES = ("dp", "tensor", "pipe")
MESH = pl.DeviceIdType.MESH
LANES = 128
DIRECT = 64


def as_column(row, rows):
    square = (rows, rows)
    diagonal = lax.broadcasted_iota(jnp.int32, square, 0) == lax.broadcasted_iota(jnp.int32, square, 1)
    return jnp.sum(jnp.where(diagonal, jnp.broadcast_to(row, square), 0.0), axis=1, keepdims=True)


def int_power(base, exponent):
    result = jnp.ones(exponent.shape, jnp.float32)
    square = jnp.full(exponent.shape, base, jnp.float32)
    for bit in range(31):
        result = jnp.where((exponent >> bit) & 1 == 1, result * square, result)
        square = square * square
    return result


def kernel(
    sizes, stages, entries, chunks,
    order_ref, step_ref, flags_ref, grad_hbm, w_hbm, m_hbm, v_hbm,
    w_out, m_out, v_out, dir_out, drop_out,
    g_bufs, w_buf, m_buf, v_buf, pair_send, pair_recv, ring_send, ring_recv,
    kept_send, kept_recv, total, red_sends, red_recvs,
    g_sem, st_sem, ps_sem, pr_sem, rs_sem, rr_sem, ks_sem, kr_sem, as_sems, ar_sems,
):
    n = sizes["dp"]
    chips = n // 2
    rows, width = w_buf.shape
    part = rows // chunks
    me = {axis: lax.axis_index(axis) for axis in AXES}
    chip, core = lax.div(me["dp"], 2), lax.rem(me["dp"], 2)

    def peer(offsets):
        return {axis: lax.rem(me[axis] + off, sizes[axis]) for axis, off in offsets.items()}

    def offsets_of(axes):
        ranges = [range(sizes[axis]) for axis in axes]
        return [dict(zip(axes, offs)) for offs in itertools.product(*ranges) if any(offs)]

    loads = []
    for k in range(chunks):
        copy = pltpu.make_async_copy(grad_hbm.at[0, 0, 0, pl.ds(k * part, part)], g_bufs[k], g_sem.at[k])
        copy.start()
        loads.append(copy)
    states = [
        pltpu.make_async_copy(src.at[0, 0], dst, st_sem.at[i])
        for i, (src, dst) in enumerate(((w_hbm, w_buf), (m_hbm, m_buf), (v_hbm, v_buf)))
    ]
    for copy in states:
        copy.start()

    barrier = pltpu.get_barrier_semaphore()
    friends = [tuple(sorted(off.items())) for axes in stages for off in offsets_of(axes)]
    friends += [tuple(sorted(off.items())) for off in offsets_of(("dp",))]
    full = [tuple(sorted({**dict.fromkeys(AXES, 0), **dict(off)}.items())) for off in friends]
    full = list(dict.fromkeys(full))
    for off in full:
        pl.semaphore_signal(barrier, inc=1, device_id=peer(dict(off)), device_id_type=MESH)

    flags_row = flags_ref[0].astype(jnp.float32)
    kept_row = 1.0 - flags_row
    kept = as_column(kept_row, rows)
    kept_send[0, :, 0:rows] = kept_row
    dropped = jnp.sum(flags_row, axis=1, keepdims=True)

    def chip_at(slot):
        return lax.rem(chip + slot, chips)

    def term(k, owner):
        block = order_ref[owner]
        picked = None
        for b in range(n):
            weight = (1 - jnp.minimum(jnp.maximum(block - b, b - block), 1)).astype(jnp.float32)
            piece = g_bufs[k][:, b * width:(b + 1) * width] * weight
            picked = piece if picked is None else picked + piece
        return picked * kept[k * part:(k + 1) * part]

    slots = list(range(1, chips)) + [0]
    for k in range(chunks):
        loads[k].wait()
        for slot in slots:
            pair_send[k, slot] = term(k, chip_at(slot) * 2 + 1 - core)

    pl.semaphore_wait(barrier, len(full))

    sibling = {"dp": chip * 2 + 1 - core}
    pair, waits = {}, []
    for group in (slots[:-1], slots[-1:]):
        for k in range(chunks):
            for slot in group:
                copy = pltpu.make_async_remote_copy(
                    pair_send.at[k, slot], pair_recv.at[k, slot],
                    ps_sem.at[k, slot], pr_sem.at[k, slot],
                    device_id=sibling, device_id_type=MESH,
                )
                copy.start()
                pair[k, slot] = copy
                waits.append(copy)
    kepts = []
    for off in range(1, n):
        copy = pltpu.make_async_remote_copy(
            kept_send.at[0], kept_recv.at[off - 1], ks_sem.at[off - 1], kr_sem.at[off - 1],
            device_id=peer({"dp": off}), device_id_type=MESH,
        )
        copy.start()
        kepts.append(copy)
        waits.append(copy)

    ring = {}
    for k in range(chunks):
        for slot in range(1, chips):
            target = chip_at(slot) * 2 + core
            mine = term(k, target)
            pair[k, slot].wait_recv()
            ring_send[k, slot - 1] = pair_recv[k, slot] + mine
            copy = pltpu.make_async_remote_copy(
                ring_send.at[k, slot - 1], ring_recv.at[k, slot - 1],
                rs_sem.at[k, slot - 1], rr_sem.at[k, slot - 1],
                device_id={"dp": target}, device_id_type=MESH,
            )
            copy.start()
            ring[k, slot] = copy
            waits.append(copy)

    count_row = kept_row
    for i, copy in enumerate(kepts):
        copy.wait_recv()
        count_row = count_row + kept_recv[i, :, 0:rows]
    inverse = 1.0 / jnp.maximum(as_column(count_row, rows), 1.0)

    for k in range(chunks):
        mine = term(k, me["dp"])
        pair[k, 0].wait_recv()
        total[k * part:(k + 1) * part, :] = pair_recv[k, 0] + mine

    steps = jnp.full((8, LANES), step_ref[0], jnp.int32)
    scale_m = (1.0 / (1.0 - int_power(0.9, steps)))[0:1, 0:1]
    scale_v = (1.0 / (1.0 - int_power(0.999, steps)))[0:1, 0:1]
    for copy in states:
        copy.wait()

    squares = jnp.zeros((8, LANES), jnp.float32)
    for k in range(chunks):
        at = slice(k * part, (k + 1) * part)
        value = total[at, :]
        for slot in range(1, chips):
            ring[k, slot].wait_recv()
            value = value + ring_recv[k, slot - 1]
        value = value * inverse[at]
        total[at, :] = value
        squares = squares + jnp.sum(
            (value * value).reshape(part // 8, 8, width // LANES, LANES), axis=(0, 2)
        )

    lane = lax.broadcasted_iota(jnp.int32, (1, LANES), 1)
    half = LANES // 2
    packed = jnp.sum(squares, axis=0, keepdims=True)
    packed = packed + pltpu.roll(packed, half, 1)
    packed = jnp.where(lane < half, packed, jnp.where(lane == half, dropped, 0.0))
    for axes, send, recv, s_sem, r_sem in zip(stages, red_sends, red_recvs, as_sems, ar_sems):
        send[0] = packed
        copies = []
        for i, off in enumerate(offsets_of(axes)):
            copy = pltpu.make_async_remote_copy(
                send.at[0], recv.at[i], s_sem.at[i], r_sem.at[i],
                device_id=peer(off), device_id_type=MESH,
            )
            copy.start()
            copies.append(copy)
            waits.append(copy)
        for i, copy in enumerate(copies):
            copy.wait_recv()
        for i in range(len(copies)):
            packed = packed + recv[i]
    square_sum = jnp.sum(jnp.where(lane < half, packed, 0.0), axis=1, keepdims=True)
    rms = jnp.sqrt(square_sum * (1.0 / entries))
    clip = jnp.minimum(1.0, 0.05 / (rms + 1e-06))

    for k in range(chunks):
        at = slice(k * part, (k + 1) * part)
        scaled = total[at, :] * clip
        new_m = 0.9 * m_buf[at, :] + 0.1 * scaled
        new_v = 0.999 * v_buf[at, :] + 0.001 * (scaled * scaled)
        weights = w_buf[at, :]
        direction = (new_m * scale_m) / (jnp.sqrt(new_v * scale_v) + 1e-08) + 0.1 * weights
        m_out[0, 0, at, :] = new_m
        v_out[0, 0, at, :] = new_v
        dir_out[0, 0, at, :] = direction
        w_out[0, 0, at, :] = weights - 0.001 * direction
    drop_out[0] = jnp.sum(jnp.where(lane == half, packed, 0.0)).astype(jnp.int32)

    for copy in waits:
        copy.wait_send()


def body(sizes, grad_parts, drop_flags, owner_order, step_count, master, moment_m, moment_v):
    n = sizes["dp"]
    chips = n // 2
    rows, columns = grad_parts.shape[-2:]
    width = master.shape[-1]
    chunks = rows // 8
    part = rows // chunks
    devices = n * sizes["tensor"] * sizes["pipe"]
    stages = [AXES] if devices <= DIRECT else [(axis,) for axis in AXES]
    peers = []
    for axes in stages:
        size = 1
        for axis in axes:
            size *= sizes[axis]
        peers.append(size - 1)
    entries = rows * columns * sizes["tensor"] * sizes["pipe"]
    padded = -(-rows // LANES) * LANES
    others = max(chips - 1, 1)
    f32 = jnp.float32
    dma = pltpu.SemaphoreType.DMA
    vmem = pl.BlockSpec(memory_space=pltpu.VMEM)
    smem = pl.BlockSpec(memory_space=pltpu.SMEM)
    hbm = pl.BlockSpec(memory_space=pl.ANY)
    state = jax.ShapeDtypeStruct(master.shape, f32)
    outs = pl.pallas_call(
        functools.partial(kernel, sizes, stages, entries, chunks),
        out_shape=(state, state, state, state, jax.ShapeDtypeStruct((1,), jnp.int32)),
        in_specs=[smem, smem, vmem, hbm, hbm, hbm, hbm],
        out_specs=(vmem, vmem, vmem, vmem, smem),
        scratch_shapes=[
            [pltpu.VMEM((part, columns), f32) for _ in range(chunks)],
            pltpu.VMEM((rows, width), f32),
            pltpu.VMEM((rows, width), f32),
            pltpu.VMEM((rows, width), f32),
            pltpu.VMEM((chunks, chips, part, width), f32),
            pltpu.VMEM((chunks, chips, part, width), f32),
            pltpu.VMEM((chunks, others, part, width), f32),
            pltpu.VMEM((chunks, others, part, width), f32),
            pltpu.VMEM((1, 1, padded), f32),
            pltpu.VMEM((n - 1, 1, padded), f32),
            pltpu.VMEM((rows, width), f32),
            [pltpu.VMEM((1, 1, LANES), f32) for _ in peers],
            [pltpu.VMEM((max(size, 1), 1, LANES), f32) for size in peers],
            dma((chunks,)),
            dma((3,)),
            dma((chunks, chips)),
            dma((chunks, chips)),
            dma((chunks, others)),
            dma((chunks, others)),
            dma((n - 1,)),
            dma((n - 1,)),
            [dma((max(size, 1),)) for size in peers],
            [dma((max(size, 1),)) for size in peers],
        ],
        compiler_params=pltpu.CompilerParams(collective_id=0, has_side_effects=True),
    )(
        owner_order, step_count.reshape(1), drop_flags.reshape(drop_flags.shape[-3:]),
        grad_parts, master, moment_m, moment_v,
    )
    return (*outs[:4], outs[4].reshape(()))


def solution(mesh):
    return jax.shard_map(
        functools.partial(body, dict(mesh.shape)),
        mesh=mesh,
        in_specs=(
            P("dp", "pipe", "tensor", None, None),
            P("dp", "pipe", "tensor", None),
            P(),
            P(),
            P("pipe", "tensor", None, "dp"),
            P("pipe", "tensor", None, "dp"),
            P("pipe", "tensor", None, "dp"),
        ),
        out_specs=(
            P("pipe", "tensor", None, "dp"),
            P("pipe", "tensor", None, "dp"),
            P("pipe", "tensor", None, "dp"),
            P("pipe", "tensor", None, "dp"),
            P(),
        ),
        check_vma=False,
    )
```

time: 92.3 us -> 36.9 us (0.40)
  blocking collectives: 67.3 us -> 0 us
  Pallas kernels: 0 us -> 28.3 us
  other arithmetic: 10.7 us -> 0 us
  starting transfers between devices: 4.26 us -> 0 us
  between operations: 4.63 us -> 2.98 us
    psum x2 -> x0, blocking collectives: 67.3 us -> none  [the longest x1 41.6 us: body(): lax.psum((jnp.sum(grad * grad), jnp.sum(flags).astype(jnp.float32)), ('dp...]
    pallas_call x0 -> x1, Pallas kernels: none -> 28.3 us  [body(): pl.pallas_call(functools.partial(kernel, sizes, stages, entries, chunks),...]
    unnamed x2 -> x8, local copies, waits for them, and re-layouts: 0.01 us -> 5.42 us
    all_to_all x1 -> x0, starting transfers between devices: 4.26 us -> none  [body(): lax.all_to_all(blocks, 'dp', split_axis=1, concat_axis=1, tiled=True)]
    sub x1 -> x0, other arithmetic: 2.86 us -> none  [body(): new_master = weights - 0.001 * direction]
    squeeze x1 -> x0, local copies, waits for them, and re-layouts: 2.67 us -> none  [body(): local_grad = grad_parts[0, 0, 0]]
    mul x1 -> x0, other arithmetic: 2.57 us -> none  [body(): term = local_grad * kept[:, None]]
    select_n x2 -> x0, other arithmetic: 2.3 us -> none  [body(): jnp.take(term.reshape(rows_here, replicas, block_cols), owner_order, axis=1)]
  transfers between devices with their start and end apart: 1 -> 0, of which waited for: 0 -> 0; matrix products, arithmetic and copies ran while one was open for 0% -> 0% of each run, Pallas kernels for 0% -> 0%
where the time goes in v1:
time: 36.9 us; the launch traced here: 36.7 us
  Pallas kernels  28.3 us (77%)
  local copies, waits for them, and re-layouts  5.42 us (15%)
  between operations  2.98 us (8%)
    pallas_call x1, Pallas kernels, body(): pl.pallas_call(functools.partial(kernel, sizes, stages, entries, chunks),...  28.3 us
    unnamed x8, local copies, waits for them, and re-layouts  5.42 us

profile of v1, /device:TPU:0, one launch (start us, length us, event | category | flops | bytes accessed | tf_op | source)
XLA Modules:
  0.0 36.7 jit_solution(13511617218435892178)
XLA Ops:
  1.3 28.3 %shard_map.110 = (f32[1,1,64,2048]{3,2,1,0:T(8,128)}, f32[1,1,64,2048]{3,2,1,0:T(8,128)}, f32[1,1,64,2048]{3,2,1,0:T(8,128)}, f32[1,1,64,2048]{3,2,1,0:T(8,128)}, s32[1]{0:T(128)}) custom-call(s32[4]{0:T(128)} %order_ref.1, s32[1]{0:T(128)} %bitcast.3.step_ref, s32[1,1,64]{2,1,0:T(1,128)} %bitcast.4, f32[1,1,1,64,8192]{4,3,2,1,0:T(8,128)} %grad_hbm.1, ...), custom_call_target="tpu_custom_call" | custom-call | tf_op jit(solution)/shard_map/pallas_call | solution.py:233
  29.6 0.0 copy-start.1
  29.6 0.0 copy-start
  29.6 2.0 %copy.18 = f32[1,1,64,2048]{3,2,1,0:T(8,128)} copy(f32[1,1,64,2048]{3,2,1,0:T(8,128)} %get-tuple-element.20) | data formatting | bytes 1048576
  31.5 1.9 %copy.19 = f32[1,1,64,2048]{3,2,1,0:T(8,128)} copy(f32[1,1,64,2048]{3,2,1,0:T(8,128)} %get-tuple-element.21) | data formatting | bytes 1048576
  33.4 0.0 copy-done.1
  33.4 0.8 %copy.20 = f32[1,1,64,2048]{3,2,1,0:T(8,128)} copy(f32[1,1,64,2048]{3,2,1,0:T(8,128)S(1)} %copy-done.1) | data formatting | bytes 1048576
  34.2 0.0 copy-done
  34.2 0.8 %copy.21 = f32[1,1,64,2048]{3,2,1,0:T(8,128)} copy(f32[1,1,64,2048]{3,2,1,0:T(8,128)S(1)} %copy-done) | data formatting | bytes 1048576
Async XLA Ops:
  29.6 3.9 %copy-start.1 = (f32[1,1,64,2048]{3,2,1,0:T(8,128)S(1)}, f32[1,1,64,2048]{3,2,1,0:T(8,128)}, u32[]{:S(2)}) copy-start(f32[1,1,64,2048]{3,2,1,0:T(8,128)} %get-tuple-element.22) | copy-start | bytes 1572868
  29.6 4.6 %copy-start = (f32[1,1,64,2048]{3,2,1,0:T(8,128)S(1)}, f32[1,1,64,2048]{3,2,1,0:T(8,128)}, u32[]{:S(2)}) copy-start(f32[1,1,64,2048]{3,2,1,0:T(8,128)} %get-tuple-element.23) | copy-start | bytes 1572868

commit v2 on v1

--- a/solution.py
+++ b/solution.py
@@ -11,6 +11,7 @@
 MESH = pl.DeviceIdType.MESH
 LANES = 128
 DIRECT = 64
+VMEM_MOST = 67043328
 
 
 def as_column(row, rows):
@@ -29,16 +30,16 @@
 
 
 def kernel(
-    sizes, stages, entries, chunks,
-    order_ref, step_ref, flags_ref, grad_hbm, w_hbm, m_hbm, v_hbm,
-    w_out, m_out, v_out, dir_out, drop_out,
-    g_bufs, w_buf, m_buf, v_buf, pair_send, pair_recv, ring_send, ring_recv,
-    kept_send, kept_recv, total, red_sends, red_recvs,
-    g_sem, st_sem, ps_sem, pr_sem, rs_sem, rr_sem, ks_sem, kr_sem, as_sems, ar_sems,
+    sizes, stages, chunks,
+    order_hbm, flags_hbm, grad_hbm,
+    total, norm_out,
+    order_ref, flags_ref, g_bufs, pair_send, pair_recv, ring_send, ring_recv,
+    kept_send, kept_recv, red_sends, red_recvs,
+    o_sem, g_sem, ps_sem, pr_sem, rs_sem, rr_sem, ks_sem, kr_sem, as_sems, ar_sems,
 ):
     n = sizes["dp"]
     chips = n // 2
-    rows, width = w_buf.shape
+    rows, width = total.shape
     part = rows // chunks
     me = {axis: lax.axis_index(axis) for axis in AXES}
     chip, core = lax.div(me["dp"], 2), lax.rem(me["dp"], 2)
@@ -50,17 +51,17 @@
         ranges = [range(sizes[axis]) for axis in axes]
         return [dict(zip(axes, offs)) for offs in itertools.product(*ranges) if any(offs)]
 
+    small = [
+        pltpu.make_async_copy(order_hbm, order_ref, o_sem.at[0]),
+        pltpu.make_async_copy(flags_hbm, flags_ref, o_sem.at[1]),
+    ]
+    for copy in small:
+        copy.start()
     loads = []
     for k in range(chunks):
         copy = pltpu.make_async_copy(grad_hbm.at[0, 0, 0, pl.ds(k * part, part)], g_bufs[k], g_sem.at[k])
         copy.start()
         loads.append(copy)
-    states = [
-        pltpu.make_async_copy(src.at[0, 0], dst, st_sem.at[i])
-        for i, (src, dst) in enumerate(((w_hbm, w_buf), (m_hbm, m_buf), (v_hbm, v_buf)))
-    ]
-    for copy in states:
-        copy.start()
 
     barrier = pltpu.get_barrier_semaphore()
     friends = [tuple(sorted(off.items())) for axes in stages for off in offsets_of(axes)]
@@ -70,6 +71,8 @@
     for off in full:
         pl.semaphore_signal(barrier, inc=1, device_id=peer(dict(off)), device_id_type=MESH)
 
+    for copy in small:
+        copy.wait()
     flags_row = flags_ref[0].astype(jnp.float32)
     kept_row = 1.0 - flags_row
     kept = as_column(kept_row, rows)
@@ -146,12 +149,6 @@
         pair[k, 0].wait_recv()
         total[k * part:(k + 1) * part, :] = pair_recv[k, 0] + mine
 
-    steps = jnp.full((8, LANES), step_ref[0], jnp.int32)
-    scale_m = (1.0 / (1.0 - int_power(0.9, steps)))[0:1, 0:1]
-    scale_v = (1.0 / (1.0 - int_power(0.999, steps)))[0:1, 0:1]
-    for copy in states:
-        copy.wait()
-
     squares = jnp.zeros((8, LANES), jnp.float32)
     for k in range(chunks):
         at = slice(k * part, (k + 1) * part)
@@ -185,25 +182,41 @@
             copy.wait_recv()
         for i in range(len(copies)):
             packed = packed + recv[i]
-    square_sum = jnp.sum(jnp.where(lane < half, packed, 0.0), axis=1, keepdims=True)
-    rms = jnp.sqrt(square_sum * (1.0 / entries))
-    clip = jnp.minimum(1.0, 0.05 / (rms + 1e-06))
-
-    for k in range(chunks):
-        at = slice(k * part, (k + 1) * part)
-        scaled = total[at, :] * clip
-        new_m = 0.9 * m_buf[at, :] + 0.1 * scaled
-        new_v = 0.999 * v_buf[at, :] + 0.001 * (scaled * scaled)
-        weights = w_buf[at, :]
-        direction = (new_m * scale_m) / (jnp.sqrt(new_v * scale_v) + 1e-08) + 0.1 * weights
-        m_out[0, 0, at, :] = new_m
-        v_out[0, 0, at, :] = new_v
-        dir_out[0, 0, at, :] = direction
-        w_out[0, 0, at, :] = weights - 0.001 * direction
-    drop_out[0] = jnp.sum(jnp.where(lane == half, packed, 0.0)).astype(jnp.int32)
+    norm_out[0] = jnp.sum(jnp.where(lane < half, packed, 0.0))
+    norm_out[1] = jnp.sum(jnp.where(lane == half, packed, 0.0))
 
     for copy in waits:
         copy.wait_send()
+
+
+def update(
+    entries, chunks, step_ref, norm_ref, grad_ref, w_ref, m_ref, v_ref,
+    w_out, m_out, v_out, dir_out, drop_out, bufs, sems,
+):
+    rows, width = grad_ref.shape
+    part = rows // chunks
+    steps = jnp.full((8, LANES), step_ref[...], jnp.int32)
+    scale_m = (1.0 / (1.0 - int_power(0.9, steps)))[0:1, 0:1]
+    scale_v = (1.0 / (1.0 - int_power(0.999, steps)))[0:1, 0:1]
+    rms = jnp.sqrt(jnp.full((8, LANES), norm_ref[0], jnp.float32) * (1.0 / entries))[0:1, 0:1]
+    clip = jnp.minimum(1.0, 0.05 / (rms + 1e-06))
+    copies = []
+    for k in range(chunks):
+        at = slice(k * part, (k + 1) * part)
+        scaled = grad_ref[at, :] * clip
+        new_m = 0.9 * m_ref[0, 0, at, :] + 0.1 * scaled
+        new_v = 0.999 * v_ref[0, 0, at, :] + 0.001 * (scaled * scaled)
+        weights = w_ref[0, 0, at, :]
+        direction = (new_m * scale_m) / (jnp.sqrt(new_v * scale_v) + 1e-08) + 0.1 * weights
+        values = (weights - 0.001 * direction, new_m, new_v, direction)
+        for i, (value, out) in enumerate(zip(values, (w_out, m_out, v_out, dir_out))):
+            bufs[i, at, :] = value
+            copy = pltpu.make_async_copy(bufs.at[i, pl.ds(k * part, part)], out.at[0, 0, pl.ds(k * part, part)], sems.at[k, i])
+            copy.start()
+            copies.append(copy)
+    drop_out[0] = norm_ref[1].astype(jnp.int32)
+    for copy in copies:
+        copy.wait()
 
 
 def body(sizes, grad_parts, drop_flags, owner_order, step_count, master, moment_m, moment_v):
@@ -228,29 +241,31 @@
     dma = pltpu.SemaphoreType.DMA
     vmem = pl.BlockSpec(memory_space=pltpu.VMEM)
     smem = pl.BlockSpec(memory_space=pltpu.SMEM)
-    hbm = pl.BlockSpec(memory_space=pl.ANY)
+    hbm = pl.BlockSpec(memory_space=pltpu.HBM)
     state = jax.ShapeDtypeStruct(master.shape, f32)
-    outs = pl.pallas_call(
-        functools.partial(kernel, sizes, stages, entries, chunks),
-        out_shape=(state, state, state, state, jax.ShapeDtypeStruct((1,), jnp.int32)),
-        in_specs=[smem, smem, vmem, hbm, hbm, hbm, hbm],
-        out_specs=(vmem, vmem, vmem, vmem, smem),
+    room = rows * columns * 4 - (64 << 10)
+    grad, norm = pl.pallas_call(
+        functools.partial(kernel, sizes, stages, chunks),
+        out_shape=(
+            jax.ShapeDtypeStruct((rows, width), f32),
+            jax.ShapeDtypeStruct((2,), f32),
+        ),
+        in_specs=[hbm, hbm, hbm],
+        out_specs=(vmem, smem),
         scratch_shapes=[
+            pltpu.SMEM((n,), jnp.int32),
+            pltpu.VMEM((1, 1, rows), jnp.int32),
             [pltpu.VMEM((part, columns), f32) for _ in range(chunks)],
-            pltpu.VMEM((rows, width), f32),
-            pltpu.VMEM((rows, width), f32),
-            pltpu.VMEM((rows, width), f32),
             pltpu.VMEM((chunks, chips, part, width), f32),
             pltpu.VMEM((chunks, chips, part, width), f32),
             pltpu.VMEM((chunks, others, part, width), f32),
             pltpu.VMEM((chunks, others, part, width), f32),
             pltpu.VMEM((1, 1, padded), f32),
             pltpu.VMEM((n - 1, 1, padded), f32),
-            pltpu.VMEM((rows, width), f32),
             [pltpu.VMEM((1, 1, LANES), f32) for _ in peers],
             [pltpu.VMEM((max(size, 1), 1, LANES), f32) for size in peers],
+            dma((2,)),
             dma((chunks,)),
-            dma((3,)),
             dma((chunks, chips)),
             dma((chunks, chips)),
             dma((chunks, others)),
@@ -260,11 +275,24 @@
             [dma((max(size, 1),)) for size in peers],
             [dma((max(size, 1),)) for size in peers],
         ],
-        compiler_params=pltpu.CompilerParams(collective_id=0, has_side_effects=True),
-    )(
-        owner_order, step_count.reshape(1), drop_flags.reshape(drop_flags.shape[-3:]),
-        grad_parts, master, moment_m, moment_v,
-    )
+        compiler_params=pltpu.CompilerParams(
+            collective_id=0, has_side_effects=True, vmem_limit_bytes=VMEM_MOST - room
+        ),
+        cost_estimate=pl.CostEstimate(
+            flops=8 * rows * columns, bytes_accessed=20 * rows * columns * 4, transcendentals=0
+        ),
+    )(owner_order, drop_flags.reshape(drop_flags.shape[-3:]), grad_parts)
+    outs = pl.pallas_call(
+        functools.partial(update, entries, chunks),
+        out_shape=(state, state, state, state, jax.ShapeDtypeStruct((1,), jnp.int32)),
+        in_specs=[smem, smem, vmem, vmem, vmem, vmem],
+        out_specs=(hbm, hbm, hbm, hbm, smem),
+        scratch_shapes=[pltpu.VMEM((4, rows, width), f32), dma((chunks, 4))],
+        compiler_params=pltpu.CompilerParams(vmem_limit_bytes=VMEM_MOST - 7 * rows * width),
+        cost_estimate=pl.CostEstimate(
+            flops=20 * rows * width, bytes_accessed=8 * rows * width * 4, transcendentals=0
+        ),
+    )(step_count, norm, grad, master, moment_m, moment_v)
     return (*outs[:4], outs[4].reshape(()))
 
 

time: 36.9 us -> 31.7 us (0.86)
  local copies, waits for them, and re-layouts: 5.42 us -> 0 us
  Pallas kernels: 28.3 us -> 30.2 us
  between operations: 2.98 us -> 1.29 us
    unnamed x8 -> x0, local copies, waits for them, and re-layouts: 5.42 us -> none
    pallas_call x1 -> x2, Pallas kernels: 28.3 us -> 30.2 us  [the longest x1 26.5 us: body(): pl.pallas_call(functools.partial(kernel, sizes, stages, chunks), out_shap...]
where the time goes in v2:
time: 31.7 us; the launch traced here: 31.5 us
  Pallas kernels  30.2 us (95%)
  between operations  1.29 us (4%)
    pallas_call x1, Pallas kernels, body(): pl.pallas_call(functools.partial(kernel, sizes, stages, chunks), out_shap...  26.5 us
    pallas_call x1, Pallas kernels, body(): pl.pallas_call(functools.partial(update, entries, chunks), out_shape=(sta...  3.73 us

profile of v2, /device:TPU:0, one launch (start us, length us, event | category | flops | bytes accessed | tf_op | source)
XLA Modules:
  0.0 31.5 jit_solution(247218576956095870)
XLA Ops:
  1.3 26.5 %shard_map.110 = (f32[64,2048]{1,0:T(8,128)}, f32[2]{0:T(128)}) custom-call(s32[4]{0:T(128)} %order_hbm.1, s32[1,1,64]{2,1,0:T(1,128)} %bitcast.2, f32[1,1,1,64,8192]{4,3,2,1,0:T(8,128)} %grad_hbm.1), custom_call_target="tpu_custom_call" | custom-call | flops 4194304 | bytes 41943040 | tf_op jit(solution)/shard_map/pallas_call | solution.py:247
  27.8 3.7 %shard_map.111 = (f32[1,1,64,2048]{3,2,1,0:T(8,128)}, f32[1,1,64,2048]{3,2,1,0:T(8,128)}, f32[1,1,64,2048]{3,2,1,0:T(8,128)}, f32[1,1,64,2048]{3,2,1,0:T(8,128)}, s32[1]{0:T(128)}) custom-call(s32[]{:T(128)S(6)} %copy.12.step_ref, f32[2]{0:T(128)} %get-tuple-element.12.norm_ref, f32[64,2048]{1,0:T(8,128)} %get-tuple-element.13.grad_ref, ...), custom_call_target="tpu_custom_call" | custom-call | flops 2621440 | bytes 4194304 | tf_op jit(solution)/shard_map/pallas_call | solution.py:285
